TPU v7x, 128 devices: a whole 4x4x4 slice. The times are simulated.
128 devices in a mesh: dp: 1, tp: 2 (over core), sp: 64 (over z, y, x).
Axes of the slice: x: 4, y: 4, z: 4, core: 2. Of those that a mesh axis runs over, the one named last changes fastest.
Arguments:
- x_in: bfloat16 [8, 4096], P('dp')
- seq_lens: int32 [8], P('dp')
- k_cache: bfloat16 [8, 4096, 32, 128], P('dp', 'sp', 'tp')
- v_cache: bfloat16 [8, 4096, 32, 128], P('dp', 'sp', 'tp')
- ln1_gain: float32 [4096], replicated
- w_qkv: bfloat16 [4096, 3, 32, 128], P(None, None, 'tp')
- w_out: bfloat16 [32, 128, 4096], P('tp')
- ln2_gain: float32 [4096], replicated
- w_up: bfloat16 [4096, 16384], P(None, 'tp')
- w_down: bfloat16 [16384, 4096], P('tp')
Outputs:
- output 1: bfloat16 [8, 4096], P('dp')
- output 2: bfloat16 [8, 4096, 32, 128], P('dp', 'sp', 'tp')
- output 3: bfloat16 [8, 4096, 32, 128], P('dp', 'sp', 'tp')
All inputs are finite; a program needn't handle non-finite values.
Results may differ from a plain program's by a relative error of at most 0.00690939.
Values sent between devices are 32-bit elements.
A program may use at most 1 GiB of HBM per device.

v0:
```python
import jax
import jax.numpy as jnp
from jax import lax
from jax.sharding import PartitionSpec as P

LN_EPS = 1e-5


def layer_norm(x_f32, gain):
    mean = jnp.mean(x_f32, axis=-1, keepdims=True)
    centred = x_f32 - mean
    variance = jnp.mean(centred * centred, axis=-1, keepdims=True)
    return centred * lax.rsqrt(variance + LN_EPS) * gain


def solution(mesh):
    tp_size = mesh.shape["tp"]

    def local_layer(x_in, seq_lens, k_cache, v_cache, ln1_gain, w_qkv, w_out, ln2_gain, w_up, w_down):
        tok_dev = k_cache.shape[1]
        local_heads = k_cache.shape[2]
        head_dim = k_cache.shape[3]
        heads = local_heads * tp_size
        tp_index = lax.axis_index("tp")
        sp_index = lax.axis_index("sp")
        normed = layer_norm(x_in.astype(jnp.float32), ln1_gain).astype(jnp.bfloat16)
        qkv_proj = jnp.einsum("bd,dchk->bchk", normed, w_qkv, preferred_element_type=jnp.float32).astype(jnp.bfloat16)
        slot_pos = sp_index * tok_dev + jnp.arange(tok_dev)
        slot_hit = (slot_pos[None, :] == seq_lens[:, None])[:, :, None, None]
        k_next = jnp.where(slot_hit, qkv_proj[:, 1][:, None], k_cache)
        v_next = jnp.where(slot_hit, qkv_proj[:, 2][:, None], v_cache)
        head_ids = tp_index * local_heads + jnp.arange(local_heads)
        slopes = jnp.exp2(-8.0 * (head_ids + 1).astype(jnp.float32) / heads)
        scores = jnp.einsum("bhk,bthk->bht", qkv_proj[:, 0], k_next, preferred_element_type=jnp.float32) * head_dim ** -0.5
        distance = (seq_lens[:, None] - slot_pos[None, :]).astype(jnp.float32)
        scores = scores - slopes[None, :, None] * distance[:, None, :]
        is_valid = (slot_pos[None, :] <= seq_lens[:, None])[:, None, :]
        scores = jnp.where(is_valid, scores, -1e30)
        local_max = jnp.max(scores, axis=2)
        weights = jnp.where(is_valid, jnp.exp(scores - local_max[:, :, None]), 0.0)
        local_sum = jnp.sum(weights, axis=2)
        local_out = jnp.einsum("bht,bthk->bhk", weights.astype(jnp.bfloat16), v_next, preferred_element_type=jnp.float32)
        global_max = lax.pmax(local_max, "sp")
        rescale = jnp.exp(local_max - global_max)
        packed = jnp.concatenate([local_out * rescale[:, :, None], (local_sum * rescale)[:, :, None]], axis=2)
        packed = lax.psum(packed, "sp")
        attended = (packed[:, :, :head_dim] / packed[:, :, head_dim:]).astype(jnp.bfloat16)
        attn_part = jnp.einsum("bhk,hkd->bd", attended, w_out, preferred_element_type=jnp.float32)
        residual = x_in.astype(jnp.float32) + lax.psum(attn_part, "tp")
        normed_mid = layer_norm(residual, ln2_gain).astype(jnp.bfloat16)
        hidden = jax.nn.gelu(jnp.dot(normed_mid, w_up, preferred_element_type=jnp.float32), approximate=False).astype(jnp.bfloat16)
        down_part = jnp.dot(hidden, w_down, preferred_element_type=jnp.float32)
        x_out = (residual + lax.psum(down_part, "tp")).astype(jnp.bfloat16)
        return x_out, k_next, v_next

    cache_spec = P("dp", "sp", "tp", None)
    in_specs = (P("dp", None), P("dp"), cache_spec, cache_spec, P(None), P(None, None, "tp", None), P("tp", None, None), P(None), P(None, "tp"), P("tp", None))
    out_specs = (P("dp", None), cache_spec, cache_spec)
    return jax.shard_map(local_layer, mesh=mesh, in_specs=in_specs, out_specs=out_specs, check_vma=False)
```

profile of v0, /device:TPU:1, one launch (start us, length us, event | category | flops | bytes accessed | tf_op | source)
XLA Modules:
  0.0 457.6 jit_solution(17433984011350682682)
XLA Ops:
  7.2 0.7 broadcast_compare_fusion.1
  8.0 0.7 subtract_convert_fusion
  8.7 1.0 convert_reduce_fusion
  9.7 1.1 fusion.23
  10.8 25.7 %fusion.6 = bf16[8,3,16,128]{3,0,2,1:T(8,128)(2,1)S(1)} fusion(bf16[4096,3,16,128]{3,2,1,0:T(8,128)(2,1)} %param.15, bf16[8,4096]{1,0:T(8,128)(2,1)} %param.10, f32[4096]{0:T(1024)} %param.14, f32[8]{0:T(128)S(1)} %add_rsqrt_fusion.1, f32[8]{0:T(128)S(1)} %broadcast_multiply_fusion.2), kind=kOutput, calls=%fused_computation.9 | convolution fusion | flops 402866176 | bytes 50511936 | tf_op jit(solution)/shard_map/bd,dchk->bchk/dot_general | solution.py:27
  36.6 2.3 broadcast_select_fusion
  38.9 1.3 copy-done.5
  40.2 1.2 fusion.4
  41.4 0.2 fusion.70
  41.8 153.5 %pmax.7 = f32[8,16]{1,0:T(8,128)S(1)} all-reduce(f32[8,16]{1,0:T(8,128)S(1)} %fusion.70), channel_id=1, replica_groups=mesh['dp'=1,'tp'=2,'sp'=64] {'sp'}, use_global_device_ids=true, to_apply=%region_3.4 | all-reduce | flops 128 | bytes 1024 | tf_op jit(solution)/shard_map/pmax | solution.py:43
  195.4 0.7 fusion.2
  196.2 0.7 pad_maximum_fusion
  196.9 145.7 %all-reduce.4.cloned.1.call-done = f32[8,16,129]{2,1,0:T(8,128)} async-done(((f32[8,16,129]{2,1,0:T(8,128)}), f32[8,16,129]{2,1,0:T(8,128)}) %all-reduce.4.cloned.1.call-update) | async-done | bytes 66064 | tf_op jit(solution)/shard_map/psum | solution.py:46
  342.6 0.9 slice_reduce_fusion
  343.5 0.9 fusion.59
  344.5 7.7 %convolution_bitcast_fusion = f32[8,4096]{1,0:T(8,128)} fusion(bf16[16,128,4096]{2,1,0:T(8,128)(2,1)} %param.16, bf16[8,16,128]{2,1,0:T(8,128)(2,1)S(1)} %fusion.59), kind=kOutput, calls=%fused_computation.2 | convolution fusion | flops 134217728 | bytes 16941056 | tf_op jit(solution)/shard_map/bhk,hkd->bd/dot_general | solution.py:48
  352.2 0.2 all-reduce.8.cloned.1.call-start
  352.4 23.9 %all-reduce.6.cloned.1.call-done = f32[8,4096]{1,0:T(8,128)} async-done(((f32[8,4096]{1,0:T(8,128)}), f32[8,4096]{1,0:T(8,128)}) %all-reduce.6.cloned.1.call-update) | async-done | bytes 131088 | tf_op jit(solution)/shard_map/psum | solution.py:49
  376.4 1.1 fusion.73
  377.4 1.1 multiply_reduce_fusion
  378.6 22.7 %fusion.56 = f32[8,8192]{1,0:T(8,128)S(1)} fusion(bf16[4096,8192]{1,0:T(8,128)(2,1)} %param.18, f32[4096]{0:T(1024)S(1)} %copy-done.6, f32[8]{0:T(128)S(1)} %add_rsqrt_fusion, f32[8]{0:T(128)S(1)} %broadcast_multiply_fusion.1, f32[8,4096]{1,0:T(8,128)} %all-reduce.6.cloned.1.call-done, bf16[8,4096]{1,0:T(8,128)(2,1)S(1)} %copy-done), kind=kOutput, calls=%fused_computation.72 | convolution fusion | flops 537067520 | bytes 67584064 | tf_op jit(solution)/shard_map/dot_general | solution.py:51
  401.3 23.3 %fusion.21 = f32[8,4096]{1,0:T(8,128)} fusion(bf16[8192,4096]{1,0:T(8,128)(2,1)} %param.19, f32[8,8192]{1,0:T(8,128)S(1)} %fusion.56), kind=kOutput, calls=%fused_computation.34 | convolution fusion | flops 541130752 | bytes 67502080 | tf_op jit(solution)/shard_map/dot_general | solution.py:52
  424.7 24.8 %all-reduce.8.cloned.1.call-done = f32[8,4096]{1,0:T(8,128)} async-done(((f32[8,4096]{1,0:T(8,128)}), f32[8,4096]{1,0:T(8,128)}) %all-reduce.8.cloned.1.call-update) | async-done | bytes 131088 | tf_op jit(solution)/shard_map/psum | solution.py:53
  449.5 1.6 add_convert_fusion
  (31 shorter events, 0.6 us)
Async XLA Ops:
  7.2 335.5 %all-reduce.4.cloned.1.call-start = ((), (), s32[]{:S(2)}) async-start(), calls=%async_computation | async-start | bytes 262144 | tf_op jit(solution)/shard_map/psum | solution.py:46
  10.8 25.8 %copy-start.2 = (bf16[8,64,16,128]{3,2,1,0:T(8,128)(2,1)S(1)}, bf16[8,64,16,128]{3,2,1,0:T(8,128)(2,1)}, u32[]{:S(2)}) copy-start(bf16[8,64,16,128]{3,2,1,0:T(8,128)(2,1)} %param.13) | copy-start | bytes 6291460
  10.8 25.8 %copy-start.3 = (bf16[8,64,16,128]{3,2,1,0:T(8,128)(2,1)S(1)}, bf16[8,64,16,128]{3,2,1,0:T(8,128)(2,1)}, u32[]{:S(2)}) copy-start(bf16[8,64,16,128]{3,2,1,0:T(8,128)(2,1)} %param.12) | copy-start | bytes 6291460
  38.9 1.3 copy-start.5
  38.9 156.5 %copy-start.4 = (bf16[8,64,16,128]{3,2,1,0:T(8,128)(2,1)S(1)}, bf16[8,64,16,128]{3,2,1,0:T(8,128)(2,1)}, u32[]{:S(2)}) copy-start(bf16[8,64,16,128]{3,2,1,0:T(8,128)(2,1)} %get-tuple-element.10) | copy-start | bytes 6291460
  196.9 179.5 %all-reduce.6.cloned.1.call-start = ((), (), s32[]{:S(2)}) async-start(), calls=%async_computation.1 | async-start | bytes 262144 | tf_op jit(solution)/shard_map/psum | solution.py:49
  344.5 31.9 %copy-start = (bf16[8,4096]{1,0:T(8,128)(2,1)S(1)}, bf16[8,4096]{1,0:T(8,128)(2,1)}, u32[]{:S(2)}) copy-start(bf16[8,4096]{1,0:T(8,128)(2,1)} %param.10) | copy-start | bytes 196612
  344.5 34.1 %copy-start.6 = (f32[4096]{0:T(1024)S(1)}, f32[4096]{0:T(1024)}, u32[]{:S(2)}) copy-start(f32[4096]{0:T(1024)} %param.17) | copy-start | bytes 49156
  352.2 97.3 %all-reduce.8.cloned.1.call-start = ((), (), s32[]{:S(2)}) async-start(), calls=%async_computation.2 | async-start | bytes 262144 | tf_op jit(solution)/shard_map/psum | solution.py:53
  401.3 48.2 %copy-start.1 = (f32[8,4096]{1,0:T(8,128)S(1)}, f32[8,4096]{1,0:T(8,128)}, u32[]{:S(2)}) copy-start(f32[8,4096]{1,0:T(8,128)} %all-reduce.6.cloned.1.call-done) | copy-start | bytes 393220
Sparse Core Ops, SparseCore 0:
  197.0 145.5 all-reduce.3
  352.3 24.0 all-reduce.5
  424.8 24.6 all-reduce.7
where the time goes:
time: 458 us
  waiting for transfers between devices  195 us (43%)
  blocking collectives  153 us (33%)
  matrix products  81.3 us (18%)
  between operations  13.9 us (3%)
  other arithmetic  11.6 us (3%)
    pmax x1, blocking collectives, local_layer(): global_max = lax.pmax(local_max, 'sp')  153 us
    psum x1, waiting for transfers between devices, local_layer(): packed = lax.psum(packed, 'sp')  146 us
    dot_general x1, matrix products, local_layer(): jnp.einsum('bd,dchk->bchk', normed, w_qkv, preferred_element_type=jnp.flo...  25.7 us
    psum x1, waiting for transfers between devices, local_layer(): x_out = (residual + lax.psum(down_part, 'tp')).astype(jnp.bfloat16)  24.8 us
    psum x1, waiting for transfers between devices, local_layer(): residual = x_in.astype(jnp.float32) + lax.psum(attn_part, 'tp')  23.9 us
    dot_general x1, matrix products, local_layer(): down_part = jnp.dot(hidden, w_down, preferred_element_type=jnp.float32)  23.3 us
    dot_general x1, matrix products, local_layer(): jnp.dot(normed_mid, w_up, preferred_element_type=jnp.float32)  22.7 us
  transfers between devices with their start and end apart: 3, of which 3 were waited for; matrix products, arithmetic and copies ran while one was open for 0% of the time, Pallas kernels for 0%

commit v1 on v0

v1 whole, which is shorter than its diff:
```python
import functools

import jax
import jax.numpy as jnp
from jax import lax
from jax.experimental import pallas as pl
from jax.experimental.pallas import tpu as pltpu
from jax.sharding import PartitionSpec as P

LN_EPS = 1e-5
MESH = pl.DeviceIdType.MESH
F32 = jnp.float32
BF16 = jnp.bfloat16

BATCH, D, HEADS, HD, TOK = 8, 4096, 16, 128, 64
FF_DEV = 1024
CHUNK = 256
N_CHUNKS = D // CHUNK
AHEAD = 6


def hops(o):
    return sum(min(d, 4 - d) for d in o)


FAR = sorted([(a, b, c) for a in range(4) for b in range(4) for c in range(4) if a + b + c], key=lambda o: -hops(o))
CUBE = sorted([(a, b, c, t) for a in range(2) for b in range(2) for c in range(2) for t in range(2) if a + b + c + t], key=lambda o: -sum(o))


def layer_norm(x, gain):
    mean = jnp.mean(x, axis=-1, keepdims=True)
    centred = x - mean
    variance = jnp.mean(centred * centred, axis=-1, keepdims=True)
    return centred * lax.rsqrt(variance + LN_EPS) * gain


def flip(v):
    return v + 1 - 2 * lax.rem(v, 2)


def kernel(
    lens, x_hbm, g1_hbm, g2_hbm, wqkv, kc, vc, wout, wup, wdown,
    x_out, k_new, v_new,
    x_v, g1_v, g2_v, ring, kc_v, vc_v, wout_v, wup_v, wdown_v,
    xrep, q_s, kv_s, kv_o, send, rs, my_o, ag, lhs_s, r_part, r_other, r_s, d_part, frs, fmine, fag,
    sem_in, sem_ring, sem_w, sem_send, sem_recv,
):
    sp = lax.axis_index("sp")
    tp = lax.axis_index("tp")
    z, y, x = sp // 16, lax.rem(sp // 4, 4), lax.rem(sp, 4)

    def far(o):
        return (lax.rem(z + o[0], 4) * 4 + lax.rem(y + o[1], 4)) * 4 + lax.rem(x + o[2], 4)

    def near(o):
        zz = flip(z) if o[0] else z
        yy = flip(y) if o[1] else y
        xx = flip(x) if o[2] else x
        block = ((lax.rem(zz, 2) * 2 + lax.rem(yy, 2)) * 2 + lax.rem(xx, 2)) * 2
        tt = 1 - tp if o[3] else tp
        return (zz * 4 + yy) * 4 + xx, tt, block + tt

    def dev(s, t):
        return (0, t, s)

    pos = (lax.rem(z, 2) * 2 + lax.rem(y, 2)) * 2 + lax.rem(x, 2)
    block = pos * 2 + tp
    group = lax.rem(x, 2)
    pair = sp // 2
    x_mate = sp + 1 - 2 * group

    def q_copy(i):
        return pltpu.make_async_copy(wqkv.at[pl.ds(i * CHUNK, CHUNK), pl.ds(0, 16)], ring.at[i], sem_ring.at[i])

    def kv_copies(i):
        return [
            pltpu.make_async_copy(
                wqkv.at[pl.ds(i * CHUNK, CHUNK), pl.ds(16 * c + 16 + 8 * group, 8)],
                ring.at[i, :, pl.ds(8 * c, 8)],
                sem_ring.at[i],
            )
            for c in range(2)
        ]

    in_x = pltpu.make_async_copy(x_hbm, x_v, sem_in.at[0])
    in_g1 = pltpu.make_async_copy(g1_hbm, g1_v, sem_in.at[1])
    in_g2 = pltpu.make_async_copy(g2_hbm, g2_v, sem_in.at[2])
    in_k = pltpu.make_async_copy(kc, kc_v, sem_in.at[3])
    in_v = pltpu.make_async_copy(vc, vc_v, sem_in.at[4])
    in_x.start()
    in_g1.start()
    for i in range(AHEAD):
        q_copy(i).start()

    barrier = pltpu.get_barrier_semaphore()
    for o in FAR:
        pl.semaphore_signal(barrier, inc=1, device_id=dev(far(o), tp), device_id_type=MESH)
    for o in CUBE:
        if o[3]:
            s, t, _ = near(o)
            pl.semaphore_signal(barrier, inc=1, device_id=dev(s, t), device_id_type=MESH)

    row = lax.broadcasted_iota(jnp.int32, (128, 2048), 0)
    col = lax.broadcasted_iota(jnp.int32, (128, 2048), 1)
    spread = jnp.where(row == col // 16, 1.0, 0.0).astype(BF16)
    in_x.wait()
    in_g1.wait()
    normed = layer_norm(x_v[...].astype(F32), g1_v[...])
    stacked = jnp.concatenate([normed[:, i * 128:(i + 1) * 128] for i in range(32)], axis=0).astype(BF16)
    rep = jnp.dot(stacked, spread, preferred_element_type=F32)
    for i in range(32):
        part = rep[i * 8:(i + 1) * 8]
        xrep[i] = jnp.concatenate([part, part], axis=0).astype(BF16)

    r16 = lax.broadcasted_iota(jnp.int32, (16, 128), 0)
    l16 = lax.rem(lax.broadcasted_iota(jnp.int32, (16, 128), 1), 16)
    masks = []
    for hp in range(8):
        m = jnp.where(l16 == 2 * hp + r16 // 8, 1.0, 0.0).astype(BF16)
        masks.append(jnp.concatenate([m] * 16, axis=1))

    def project(i, acc):
        for half in range(2):
            xx = xrep[i * 2 + half]
            lhs = jnp.concatenate([xx * m for m in masks], axis=0)
            rhs = ring[i, half * 128:(half + 1) * 128].reshape(2048, 128)
            acc = acc + jnp.dot(lhs, rhs, preferred_element_type=F32)
        return acc

    def q_step(i, acc):
        q_copy(i).wait()

        @pl.when(i < N_CHUNKS - AHEAD)
        def _():
            q_copy(i + AHEAD).start()

        @pl.when(i == N_CHUNKS - AHEAD)
        def _():
            in_k.start()
            in_v.start()

        @pl.when(i >= N_CHUNKS - AHEAD)
        def _():
            for c in kv_copies(i - (N_CHUNKS - AHEAD)):
                c.start()

        return project(i, acc)

    q = lax.fori_loop(0, N_CHUNKS, q_step, jnp.zeros((128, 128), F32))
    q_s[...] = q.astype(BF16).astype(F32).reshape(16, 8, 128)

    for i in range(AHEAD, N_CHUNKS):
        for c in kv_copies(i):
            c.start()

    hrow = lax.broadcasted_iota(jnp.int32, (16, 1024), 0)
    lane = lax.broadcasted_iota(jnp.int32, (16, 1024), 1)
    own = hrow == lax.rem(lane, 16)
    slot = sp * TOK + lane // 16
    slope = jnp.exp2(-8.0 * (tp * 16 + hrow[:, :128] + 1).astype(F32) / 32.0)
    slope = jnp.concatenate([slope] * 8, axis=1)
    low = lax.broadcasted_iota(jnp.int32, (16, 128), 1) < 64
    in_k.wait()
    in_v.wait()
    for b in range(BATCH):
        qb = q_s[:, b, :].astype(BF16)
        s = lax.dot_general(qb, kc_v[b], (((1,), (1,)), ((), ())), preferred_element_type=F32) * HD ** -0.5
        length = lens[b]
        s = s - slope * (length - slot).astype(F32)
        valid = own & (slot < length)
        s = jnp.where(valid, s, -1e30)
        m = jnp.max(s, axis=1, keepdims=True)
        p = jnp.where(valid, jnp.exp(s - m), 0.0)
        l = jnp.sum(p, axis=1, keepdims=True)
        o = jnp.dot(p.astype(BF16), vc_v[b], preferred_element_type=F32)
        ml = jnp.where(low, m, l)
        for h in range(16):
            to = (h % 8) * 8 + (b // 2) * 2 + h // 8
            send[to, b % 2:b % 2 + 1, :] = o[h:h + 1]
            send[to, 2 + b % 2:3 + b % 2, :] = ml[h:h + 1]

    pl.semaphore_wait(barrier, len(FAR) + 8)
    rs[sp] = send[sp]
    for o in FAR:
        s = far(o)
        pltpu.make_async_remote_copy(
            src_ref=send.at[s], dst_ref=rs.at[sp], send_sem=sem_send.at[0], recv_sem=sem_recv.at[0],
            device_id=dev(s, tp), device_id_type=MESH,
        ).start()

    def kv_step(i, acc):
        for c in kv_copies(i):
            c.wait()
        pltpu.make_async_copy(wout.at[pl.ds(i * 128, 128)], wout_v.at[pl.ds(i * 128, 128)], sem_w.at[0]).start()
        return project(i, acc)

    kv = lax.fori_loop(0, N_CHUNKS, kv_step, jnp.zeros((128, 128), F32))
    in_g2.start()
    for i in range(8):
        pltpu.make_async_copy(wup.at[pl.ds(i * 512, 512), pl.ds(pos * FF_DEV, FF_DEV)], wup_v.at[pl.ds(i * 512, 512)], sem_w.at[1]).start()
    for i in range(8):
        pltpu.make_async_copy(wdown.at[pl.ds(pos * FF_DEV + i * 128, 128)], wdown_v.at[pl.ds(i * 128, 128)], sem_w.at[2]).start()
    kv_s[...] = kv.astype(BF16).astype(F32).reshape(16, 8, 128)
    kv_send = pltpu.make_async_remote_copy(
        src_ref=kv_s, dst_ref=kv_o, send_sem=sem_send.at[1], recv_sem=sem_recv.at[1],
        device_id=dev(x_mate, tp), device_id_type=MESH,
    )
    kv_send.start()

    head8 = pair // 4
    first = 2 * lax.rem(pair, 4)
    turn = lax.rem(8 - first, 8)
    row8 = lax.broadcasted_iota(jnp.int32, (8, 128), 0)

    def pick(v):
        v = pltpu.roll(v, turn, 0)
        return jnp.where(row8 < 4, v, pltpu.roll(v, 4, 0))

    s_new = jnp.sum(q_s[group * 8 + head8] * kv_s[head8], axis=1, keepdims=True) * HD ** -0.5
    s_new = pick(jnp.broadcast_to(s_new, (8, 128)))
    v_mine = pick(kv_s[8 + head8])

    def wait_recv(buf, n, k):
        pltpu.make_async_copy(buf.at[pl.ds(0, n)], buf.at[pl.ds(0, n)], sem_recv.at[k]).wait()

    def wait_send(buf, n, k):
        pltpu.make_async_copy(buf.at[pl.ds(0, n)], buf.at[pl.ds(0, n)], sem_send.at[k]).wait()

    wait_recv(rs, 63, 0)
    got = rs[...].reshape(256, 128)
    ml = pltpu.roll(got, 254, 0)
    swapped = pltpu.roll(ml, 64, 1)
    lowg = lax.broadcasted_iota(jnp.int32, (256, 128), 1) < 64
    m = jnp.where(lowg, ml, swapped).reshape(32, 8, 128)
    l = jnp.where(lowg, swapped, ml).reshape(32, 8, 128)
    top = jnp.max(m, axis=0)
    top = jnp.maximum(jnp.maximum(top, pltpu.roll(top, 4, 0)), s_new)
    w = jnp.exp(m - top[None])
    o_sum = jnp.sum(w * got.reshape(32, 8, 128), axis=0)
    l_sum = jnp.sum(w * l, axis=0)
    w_new = jnp.exp(s_new - top)
    o_sum = o_sum + pltpu.roll(o_sum, 4, 0) + w_new * v_mine
    l_sum = l_sum + pltpu.roll(l_sum, 4, 0) + w_new
    mine = (o_sum / l_sum)[:2]
    my_o[...] = mine
    ag[sp] = mine
    for o in FAR:
        pltpu.make_async_remote_copy(
            src_ref=my_o, dst_ref=ag.at[sp], send_sem=sem_send.at[2], recv_sem=sem_recv.at[2],
            device_id=dev(far(o), tp), device_id_type=MESH,
        ).start()

    kv_send.wait_recv()
    for h8 in range(8):
        for c, ref in ((0, k_new), (1, v_new)):
            a, b = kv_s[8 * c + h8], kv_o[8 * c + h8]
            ref[:, h8, :] = jnp.where(group == 0, a, b)
            ref[:, 8 + h8, :] = jnp.where(group == 0, b, a)
    pltpu.make_async_copy(wout, wout_v, sem_w.at[0]).wait()

    wait_recv(ag, 63, 2)
    for s in range(64):
        h, b2 = (s % 2) * 8 + s // 8, (s // 2) % 4
        lhs_s[h, 2 * b2:2 * b2 + 2, :] = ag[s]
    lhs = jnp.concatenate([lhs_s[h] for h in range(16)], axis=1).astype(BF16)

    def out_step(n, c):
        cols = pl.ds(pl.multiple_of(n * 512, 512), 512)
        r_part[:, cols] = jnp.dot(lhs, wout_v[:, cols], preferred_element_type=F32)
        return c

    lax.fori_loop(0, 8, out_step, 0)
    r_send = pltpu.make_async_remote_copy(
        src_ref=r_part, dst_ref=r_other, send_sem=sem_send.at[3], recv_sem=sem_recv.at[3],
        device_id=dev(sp, 1 - tp), device_id_type=MESH,
    )
    r_send.start()
    in_g2.wait()
    r_send.wait_recv()
    r = x_v[...].astype(F32) + (r_part[...] + r_other[...])
    for j in range(16):
        r_s[j] = r[:, j * 256:(j + 1) * 256]
    mid = layer_norm(r, g2_v[...]).astype(BF16)
    pltpu.make_async_copy(wup.at[:, pl.ds(0, FF_DEV)], wup_v, sem_w.at[1]).wait()
    up = jnp.concatenate(
        [jnp.dot(mid, wup_v[:, n * 256:(n + 1) * 256], preferred_element_type=F32) for n in range(FF_DEV // 256)], axis=1)
    hidden = (0.5 * up * (1.0 + lax.erf(up * 0.5 ** 0.5))).astype(BF16)
    pltpu.make_async_copy(wdown.at[pl.ds(0, FF_DEV)], wdown_v, sem_w.at[2]).wait()
    for j in range(16):
        d_part[j] = jnp.dot(hidden, wdown_v[:, j * 256:(j + 1) * 256], preferred_element_type=F32)
    frs[block] = d_part[block]
    for o in CUBE:
        s, t, to = near(o)
        pltpu.make_async_remote_copy(
            src_ref=d_part.at[to], dst_ref=frs.at[block], send_sem=sem_send.at[4], recv_sem=sem_recv.at[4],
            device_id=dev(s, t), device_id_type=MESH,
        ).start()
    wait_recv(frs, 15, 4)
    done = (r_s[block] + jnp.sum(frs[...], axis=0)).astype(BF16).astype(F32)
    fmine[...] = done
    fag[block] = done
    for o in CUBE:
        s, t, _ = near(o)
        pltpu.make_async_remote_copy(
            src_ref=fmine, dst_ref=fag.at[block], send_sem=sem_send.at[5], recv_sem=sem_recv.at[5],
            device_id=dev(s, t), device_id_type=MESH,
        ).start()
    wait_send(send, 63, 0)
    kv_send.wait_send()
    wait_send(ag, 63, 2)
    r_send.wait_send()
    wait_send(d_part, 15, 4)
    wait_recv(fag, 15, 5)
    for j in range(16):
        x_out[:, j * 256:(j + 1) * 256] = fag[j].astype(BF16)
    wait_send(fag, 15, 5)


def solution(mesh):
    def local_layer(x_in, seq_lens, k_cache, v_cache, ln1_gain, w_qkv, w_out, ln2_gain, w_up, w_down):
        any_spec = pl.BlockSpec(memory_space=pl.ANY)
        vmem = pl.BlockSpec(memory_space=pltpu.VMEM)
        x_out, k_new, v_new = pl.pallas_call(
            kernel,
            out_shape=(
                jax.ShapeDtypeStruct((BATCH, D), BF16),
                jax.ShapeDtypeStruct((BATCH, 16, 128), F32),
                jax.ShapeDtypeStruct((BATCH, 16, 128), F32),
            ),
            in_specs=[pl.BlockSpec(memory_space=pltpu.SMEM)] + [any_spec] * 9,
            out_specs=(vmem, vmem, vmem),
            scratch_shapes=[
                pltpu.VMEM((BATCH, D), BF16),
                pltpu.VMEM((1, D), F32),
                pltpu.VMEM((1, D), F32),
                pltpu.VMEM((N_CHUNKS, CHUNK, 16, 128), BF16),
                pltpu.VMEM((BATCH, 1024, 128), BF16),
                pltpu.VMEM((BATCH, 1024, 128), BF16),
                pltpu.VMEM((2048, D), BF16),
                pltpu.VMEM((D, FF_DEV), BF16),
                pltpu.VMEM((FF_DEV, D), BF16),
                pltpu.VMEM((32, 16, 2048), BF16),
                pltpu.VMEM((16, 8, 128), F32),
                pltpu.VMEM((16, 8, 128), F32),
                pltpu.VMEM((16, 8, 128), F32),
                pltpu.VMEM((64, 4, 128), F32),
                pltpu.VMEM((64, 4, 128), F32),
                pltpu.VMEM((2, 128), F32),
                pltpu.VMEM((64, 2, 128), F32),
                pltpu.VMEM((16, 8, 128), F32),
                pltpu.VMEM((BATCH, D), F32),
                pltpu.VMEM((BATCH, D), F32),
                pltpu.VMEM((16, 8, 256), F32),
                pltpu.VMEM((16, 8, 256), F32),
                pltpu.VMEM((16, 8, 256), F32),
                pltpu.VMEM((8, 256), F32),
                pltpu.VMEM((16, 8, 256), F32),
                pltpu.SemaphoreType.DMA((5,)),
                pltpu.SemaphoreType.DMA((N_CHUNKS,)),
                pltpu.SemaphoreType.DMA((3,)),
                pltpu.SemaphoreType.DMA((6,)),
                pltpu.SemaphoreType.DMA((6,)),
            ],
            compiler_params=pltpu.CompilerParams(
                collective_id=0, has_side_effects=True, vmem_limit_bytes=67043328),
            name="layer",
        )(
            seq_lens, x_in, ln1_gain.reshape(1, D), ln2_gain.reshape(1, D), w_qkv.reshape(D, 48, 128),
            k_cache.reshape(BATCH, 1024, 128), v_cache.reshape(BATCH, 1024, 128), w_out.reshape(2048, D), w_up, w_down,
        )
        slot_pos = lax.axis_index("sp") * TOK + jnp.arange(TOK)
        slot_hit = (slot_pos[None, :] == seq_lens[:, None])[:, :, None, None]
        k_next = jnp.where(slot_hit, k_new.astype(BF16)[:, None], k_cache)
        v_next = jnp.where(slot_hit, v_new.astype(BF16)[:, None], v_cache)
        return x_out, k_next, v_next

    cache_spec = P("dp", "sp", "tp", None)
    in_specs = (P("dp", None), P("dp"), cache_spec, cache_spec, P(None), P(None, None, "tp", None), P("tp", None, None), P(None), P(None, "tp"), P("tp", None))
    out_specs = (P("dp", None), cache_spec, cache_spec)
    return jax.shard_map(local_layer, mesh=mesh, in_specs=in_specs, out_specs=out_specs, check_vma=False)
```

time: 458 us -> 56.3 us (0.12)
  waiting for transfers between devices: 195 us -> 0 us
  blocking collectives: 153 us -> 0 us
  matrix products: 81.3 us -> 0 us
  Pallas kernels: 0 us -> 47.8 us
  between operations: 13.9 us -> 0.65 us
  other arithmetic: 11.6 us -> 6.93 us
    psum x3 -> x0, waiting for transfers between devices: 194 us -> none  [the longest x1 146 us: local_layer(): packed = lax.psum(packed, 'sp')]
    pmax x1 -> x0, blocking collectives: 153 us -> none  [local_layer(): global_max = lax.pmax(local_max, 'sp')]
    dot_general x6 -> x0, matrix products: 81.3 us -> none  [the longest x1 25.7 us: local_layer(): jnp.einsum('bd,dchk->bchk', normed, w_qkv, preferred_element_type=jnp.flo...]
    pallas_call x0 -> x1, Pallas kernels: none -> 47.8 us  [local_layer(): pl.pallas_call(kernel, out_shape=(jax.ShapeDtypeStruct((BATCH, D), BF16),...]
  transfers between devices with their start and end apart: 3 -> 0, of which waited for: 3 -> 0; matrix products, arithmetic and copies ran while one was open for 0% -> 0% of each run, Pallas kernels for 0% -> 0%
where the time goes in v1:
time: 56.3 us; the launch traced here: 56.1 us
  Pallas kernels  47.8 us (85%)
  other arithmetic  6.93 us (12%)
  between operations  0.65 us (1%)
  local copies, waits for them, and re-layouts  0.63 us (1%)
    pallas_call x1, Pallas kernels, local_layer(): pl.pallas_call(kernel, out_shape=(jax.ShapeDtypeStruct((BATCH, D), BF16),...  47.8 us
    select_n x1, other arithmetic, local_layer(): v_next = jnp.where(slot_hit, v_new.astype(BF16)[:, None], v_cache)  3.95 us
    eq x1, other arithmetic, local_layer(): slot_hit = (slot_pos[None, :] == seq_lens[:, None])[:, :, None, None]  1.29 us

profile of v1, /device:TPU:1, one launch (start us, length us, event | category | flops | bytes accessed | tf_op | source)
XLA Modules:
  0.0 56.1 jit_solution(3716826466930575700)
XLA Ops:
  0.6 1.3 %broadcast_compare_fusion = pred[8,64]{1,0:T(8,128)(4,1)} fusion(s32[64]{0:T(128)S(1)} %iota_add_fusion, s32[8]{0:T(128)} %lens.1), kind=kLoop, calls=%fused_computation.2 | loop fusion | flops 512 | bytes 800 | tf_op jit(solution)/shard_map/eq | solution.py:372
  1.9 47.8 %layer.1 = (bf16[8,4096]{1,0:T(8,128)(2,1)}, f32[8,16,128]{2,1,0:T(8,128)}, f32[8,16,128]{2,1,0:T(8,128)}) custom-call(s32[8]{0:T(128)} %lens.1, bf16[8,4096]{1,0:T(8,128)(2,1)} %x_hbm.1, f32[1,4096]{1,0:T(1,128)} %bitcast.10, f32[1,4096]{1,0:T(1,128)} %bitcast.11, bf16[4096,48,128]{2,1,0:T(8,128)(2,1)} %bitcast.6, bf16[8,1024,128]{2,1,0:T(8,128)(2,1)} %bitcast.8, ...), custom_call_target="tpu_custom_call" | custom-call | tf_op jit(solution)/shard_map/layer/pallas_call | solution.py:323
  49.8 0.8 %convert_element_type.6 = bf16[8,16,128]{2,1,0:T(8,128)(2,1)S(1)} convert(f32[8,16,128]{2,1,0:T(8,128)} %get-tuple-element.7) | non-fusion elementwise | flops 16384 | bytes 98304 | tf_op jit(solution)/shard_map/convert_element_type | solution.py:373
  50.6 0.8 %convert_element_type.7 = bf16[8,16,128]{2,1,0:T(8,128)(2,1)S(1)} convert(f32[8,16,128]{2,1,0:T(8,128)} %get-tuple-element.8) | non-fusion elementwise | flops 16384 | bytes 98304 | tf_op jit(solution)/shard_map/convert_element_type | solution.py:374
  51.5 0.0 copy-start
  51.5 3.9 %broadcast_select_fusion = (bf16[8,64,16,128]{3,2,1,0:T(8,128)(2,1)}, bf16[8,64,16,128]{3,2,1,0:T(8,128)(2,1)}) fusion(bf16[8,64,16,128]{3,2,1,0:T(8,128)(2,1)} %param.13, pred[8,64]{1,0:T(8,128)(4,1)} %broadcast_compare_fusion, bf16[8,16,128]{2,1,0:T(8,128)(2,1)S(1)} %convert_element_type.7, bf16[8,64,16,128]{3,2,1,0:T(8,128)(2,1)} %param.12, ...), kind=kLoop, calls=%fused_computation | loop fusion | flops 2097152 | bytes 8454656 | tf_op jit(solution)/shard_map/jit(_where)/select_n | solution.py:374
  55.4 0.0 copy-done
  55.4 0.6 %copy.14 = bf16[8,4096]{1,0:T(8,128)(2,1)} copy(bf16[8,4096]{1,0:T(8,128)(2,1)S(1)} %copy-done) | data formatting | bytes 131072
  (1 shorter events, 0.0 us)
Async XLA Ops:
  51.5 4.0 %copy-start = (bf16[8,4096]{1,0:T(8,128)(2,1)S(1)}, bf16[8,4096]{1,0:T(8,128)(2,1)}, u32[]{:S(2)}) copy-start(bf16[8,4096]{1,0:T(8,128)(2,1)} %get-tuple-element.14) | copy-start | bytes 196612
